TPU v7x, 32 devices: a whole 2x2x4 slice. The times are simulated.
32 devices in a mesh: row: 4 (over y, core), col: 8 (over z, x).
Axes of the slice: x: 2, y: 2, z: 4, core: 2. Of those that a mesh axis runs over, the one named last changes fastest.
Arguments:
- matrix: float32 [16384, 16384], P('row', 'col'), may hold values from -500 to 500
Outputs:
- reduced: float32 [16384, 16384], P('row', 'col')
All inputs are finite; a program needn't handle non-finite values.
Results may differ from a plain program's by a relative error of at most 0.0003.
Values sent between devices are 32-bit elements; how exact they have to be, the bound alone decides.
A program may use at most 192 MiB of HBM per device.

v0:
```python
import jax
import jax.numpy as jnp
from jax import lax
from jax.sharding import PartitionSpec as P

REFL = 4
PANELS = 2


highest = lax.Precision.HIGHEST


def from_root(value, axis, source):
    kept = jnp.where(lax.axis_index(axis) == source, value, 0).astype(value.dtype)
    return lax.psum(kept, axis)


def product(left, right):
    return jnp.dot(left, right, precision=highest, preferred_element_type=jnp.float32)


def on_device(matrix):
    rows_local, cols_local = matrix.shape
    row_start = lax.axis_index("row") * rows_local
    col_start = lax.axis_index("col") * cols_local
    total = rows_local * lax.axis_size("row")
    positions = jnp.arange(total, dtype=jnp.int32)
    current = matrix
    for panel_index in range(PANELS):
        reflectors = jnp.zeros((total, REFL), jnp.float32)
        updates = jnp.zeros((total, REFL), jnp.float32)
        for inner_index in range(REFL):
            target = panel_index * REFL + inner_index
            owner = target // cols_local
            own_slice = current[:, target - owner * cols_local]
            reflector_rows = lax.dynamic_slice_in_dim(reflectors, row_start, rows_local, 0)
            update_block = lax.dynamic_slice_in_dim(updates, row_start, rows_local, 0)
            held = from_root(own_slice, "col", owner)
            column = (
                held
                - product(reflector_rows, updates[target])
                - product(update_block, reflectors[target])
            )
            whole = lax.all_gather(column, "row", axis=0, tiled=True)
            beneath = jnp.where(positions > target, whole, 0.0)
            leading = whole[target + 1]
            length = jnp.sqrt(jnp.sum(beneath * beneath))
            signed = jnp.where(leading >= 0.0, length, -length)
            vector = beneath + jnp.where(positions == target + 1, signed, 0.0)
            factor = 1.0 / (length * (length + jnp.abs(leading)))
            vector_cols = lax.dynamic_slice_in_dim(vector, col_start, cols_local, 0)
            against_updates = product(vector, updates)
            against_reflectors = product(vector, reflectors)
            summed = lax.psum(product(current, vector_cols), "col")
            mapped = factor * (
                summed
                - product(reflector_rows, against_updates)
                - product(update_block, against_reflectors)
            )
            vector_rows = lax.dynamic_slice_in_dim(vector, row_start, rows_local, 0)
            inner = lax.psum(jnp.sum(mapped * vector_rows), "row")
            update = lax.all_gather(
                mapped - 0.5 * factor * inner * vector_rows, "row", axis=0, tiled=True
            )
            reflectors = reflectors.at[:, inner_index].set(vector)
            updates = updates.at[:, inner_index].set(update)
        reflector_rows = lax.dynamic_slice_in_dim(reflectors, row_start, rows_local, 0)
        update_block = lax.dynamic_slice_in_dim(updates, row_start, rows_local, 0)
        reflector_cols = lax.dynamic_slice_in_dim(reflectors, col_start, cols_local, 0)
        update_cols = lax.dynamic_slice_in_dim(updates, col_start, cols_local, 0)
        current = (
            current
            - product(reflector_rows, update_cols.T)
            - product(update_block, reflector_cols.T)
        )
    return current


def solution(mesh):
    return jax.shard_map(
        on_device,
        mesh=mesh,
        in_specs=(P("row", "col"),),
        out_specs=P("row", "col"),
        check_vma=False,
    )
```

profile of v0, /device:TPU:0, one launch (start us, length us, event | category | flops | bytes accessed | tf_op | source)
XLA Modules:
  0.0 982.2 jit_solution(17959320532915637002)
XLA Ops:
  3.4 31.1 %copy.46 = f32[4096,2048]{0,1:T(8,128)} copy(f32[4096,2048]{1,0:T(8,128)} %param.33) | data formatting | bytes 67108864 | tf_op args[0]
  35.8 38.8 %psum.168 = f32[4096]{0:T(1024)S(1)} all-reduce(f32[4096]{0:T(1024)S(1)} %bitcast.324), channel_id=1, replica_groups=mesh['row'=4,'col'=8] {'col'}, use_global_device_ids=true, to_apply=%region_1.2 | all-reduce | flops 4096 | bytes 32768 | tf_op jit(solution)/shard_map/psum | solution.py:15
  74.7 5.2 all_gather.48
  85.9 30.7 %fusion.128 = f32[1,4096]{1,0:T(1,128)S(1)} fusion(f32[2048,1]{0,1:T(1,128)S(1)} %bitcast.325, f32[4096,2048]{1,0:T(8,128)} %param.33), kind=kOutput, calls=%fused_computation.249 | convolution fusion | flops 100663296 | bytes 33579008 | tf_op jit(solution)/shard_map/dot_general | solution.py:19
  116.6 33.1 %all-reduce.9 = (f32[4096]{0:T(1024)S(1)}, f32[4096]{0:T(1024)S(1)}) all-reduce(f32[4096]{0:T(1024)S(1)} %bitcast.289, f32[4096]{0:T(1024)S(1)} %bitcast.322), channel_id=1, replica_groups=mesh['row'=4,'col'=8] {'col'}, use_global_device_ids=true, to_apply=%region_5.6 | all-reduce | flops 8192 | bytes 65536 | tf_op jit(solution)/shard_map/psum | solution.py:54
  151.1 6.3 psum.171
  158.1 5.2 all_gather.49
  164.8 5.5 all_gather.50
  176.8 30.7 %fusion.129 = f32[1,4096]{1,0:T(1,128)S(1)} fusion(f32[2048,1]{0,1:T(1,128)S(1)} %bitcast.326, f32[4096,2048]{1,0:T(8,128)} %param.33), kind=kOutput, calls=%fused_computation.250 | convolution fusion | flops 100663296 | bytes 33579008 | tf_op jit(solution)/shard_map/dot_general | solution.py:19
  207.5 33.1 %all-reduce.8 = (f32[4096]{0:T(1024)S(1)}, f32[4096]{0:T(1024)S(1)}) all-reduce(f32[4096]{0:T(1024)S(1)} %bitcast.290, f32[4096]{0:T(1024)S(1)} %bitcast.320), channel_id=1, replica_groups=mesh['row'=4,'col'=8] {'col'}, use_global_device_ids=true, to_apply=%region_11.12 | all-reduce | flops 8192 | bytes 65536 | tf_op jit(solution)/shard_map/psum | solution.py:54
  241.8 6.3 psum.174
  248.6 5.2 all_gather.51
  257.9 5.7 all_gather.52
  269.5 30.7 %fusion.130 = f32[1,4096]{1,0:T(1,128)S(1)} fusion(f32[2048,1]{0,1:T(1,128)S(1)} %bitcast.327, f32[4096,2048]{1,0:T(8,128)} %param.33), kind=kOutput, calls=%fused_computation.251 | convolution fusion | flops 100663296 | bytes 33579008 | tf_op jit(solution)/shard_map/dot_general | solution.py:19
  300.2 33.1 %all-reduce.7 = (f32[4096]{0:T(1024)S(1)}, f32[4096]{0:T(1024)S(1)}) all-reduce(f32[4096]{0:T(1024)S(1)} %bitcast.291, f32[4096]{0:T(1024)S(1)} %bitcast.318), channel_id=1, replica_groups=mesh['row'=4,'col'=8] {'col'}, use_global_device_ids=true, to_apply=%region_16.17 | all-reduce | flops 8192 | bytes 65536 | tf_op jit(solution)/shard_map/psum | solution.py:54
  334.5 6.3 psum.177
  341.3 5.2 all_gather.53
  351.4 5.5 all_gather.54
  362.8 30.7 %fusion.131 = f32[1,4096]{1,0:T(1,128)S(1)} fusion(f32[2048,1]{0,1:T(1,128)S(1)} %bitcast.328, f32[4096,2048]{1,0:T(8,128)} %param.33), kind=kOutput, calls=%fused_computation.252 | convolution fusion | flops 100663296 | bytes 33579008 | tf_op jit(solution)/shard_map/dot_general | solution.py:19
  393.5 33.0 %psum.178 = f32[4096]{0:T(1024)S(1)} all-reduce(f32[4096]{0:T(1024)S(1)} %bitcast.292), channel_id=1, replica_groups=mesh['row'=4,'col'=8] {'col'}, use_global_device_ids=true, to_apply=%region_20.21 | all-reduce | flops 4096 | bytes 32768 | tf_op jit(solution)/shard_map/psum | solution.py:54
  428.9 6.3 psum.179
  435.7 5.4 all_gather.55
  442.3 30.1 %fusion.14 = f32[4096,2048]{0,1:T(8,128)} fusion(f32[16384,4]{0,1:T(4,128)S(1)} %scatter.64, s32[]{:T(128)S(6)} %select_n.183, f32[16384,4]{0,1:T(4,128)S(1)} %scatter.65, s32[]{:T(128)S(6)} %select_n.184), kind=kOutput, calls=%fused_computation.58 | convolution fusion | flops 402653184 | bytes 33652744 | tf_op jit(solution)/shard_map/dot_general | solution.py:19
  472.4 41.2 %subtract_subtract_fusion.1 = f32[4096,2048]{0,1:T(8,128)} fusion(f32[4096,2048]{0,1:T(8,128)} %copy.46, f32[4096,2048]{0,1:T(8,128)} %fusion.14, f32[16384,4]{0,1:T(4,128)S(1)} %scatter.65, s32[]{:T(128)S(6)} %select_n.183, f32[16384,4]{0,1:T(4,128)S(1)} %scatter.64, s32[]{:T(128)S(6)} %select_n.184), kind=kOutput, calls=%fused_computation.1 | convolution fusion | flops 419430400 | bytes 100761608 | tf_op jit(solution)/shard_map/dot_general | solution.py:19
  515.0 33.0 %psum.180 = f32[4096]{0:T(1024)S(1)} all-reduce(f32[4096]{0:T(1024)S(1)} %bitcast.323), channel_id=1, replica_groups=mesh['row'=4,'col'=8] {'col'}, use_global_device_ids=true, to_apply=%region_23.24 | all-reduce | flops 4096 | bytes 32768 | tf_op jit(solution)/shard_map/psum | solution.py:15
  548.0 5.2 all_gather.56
  559.2 21.5 %fusion.132 = f32[1,4096]{1,0:T(1,128)S(1)} fusion(f32[4096,2048]{0,1:T(8,128)} %subtract_subtract_fusion.1, f32[2048,1]{0,1:T(1,128)S(1)} %bitcast.329), kind=kOutput, calls=%fused_computation.253 | convolution fusion | flops 100663296 | bytes 33579008 | tf_op jit(solution)/shard_map/dot_general | solution.py:19
  580.7 33.1 %all-reduce.6 = (f32[4096]{0:T(1024)S(1)}, f32[4096]{0:T(1024)S(1)}) all-reduce(f32[4096]{0:T(1024)S(1)} %bitcast.285, f32[4096]{0:T(1024)S(1)} %bitcast.321), channel_id=1, replica_groups=mesh['row'=4,'col'=8] {'col'}, use_global_device_ids=true, to_apply=%region_26.27 | all-reduce | flops 8192 | bytes 65536 | tf_op jit(solution)/shard_map/psum | solution.py:54
  615.2 6.3 psum.183
  622.2 5.2 all_gather.57
  628.9 5.4 all_gather.58
  640.8 21.0 %fusion.133 = f32[1,4096]{1,0:T(1,128)S(1)} fusion(f32[4096,2048]{0,1:T(8,128)} %subtract_subtract_fusion.1, f32[2048,1]{0,1:T(1,128)S(1)} %bitcast.330), kind=kOutput, calls=%fused_computation.254 | convolution fusion | flops 100663296 | bytes 33579008 | tf_op jit(solution)/shard_map/dot_general | solution.py:19
  661.9 33.2 %all-reduce.5 = (f32[4096]{0:T(1024)S(1)}, f32[4096]{0:T(1024)S(1)}) all-reduce(f32[4096]{0:T(1024)S(1)} %bitcast.286, f32[4096]{0:T(1024)S(1)} %bitcast.319), channel_id=1, replica_groups=mesh['row'=4,'col'=8] {'col'}, use_global_device_ids=true, to_apply=%region_31.32 | all-reduce | flops 8192 | bytes 65536 | tf_op jit(solution)/shard_map/psum | solution.py:54
  696.3 6.3 psum.186
  703.2 5.2 all_gather.59
  712.4 5.3 all_gather.60
  723.6 21.0 %fusion.134 = f32[1,4096]{1,0:T(1,128)S(1)} fusion(f32[4096,2048]{0,1:T(8,128)} %subtract_subtract_fusion.1, f32[2048,1]{0,1:T(1,128)S(1)} %bitcast.331), kind=kOutput, calls=%fused_computation.255 | convolution fusion | flops 100663296 | bytes 33579008 | tf_op jit(solution)/shard_map/dot_general | solution.py:19
  744.7 33.1 %all-reduce.4 = (f32[4096]{0:T(1024)S(1)}, f32[4096]{0:T(1024)S(1)}) all-reduce(f32[4096]{0:T(1024)S(1)} %bitcast.287, f32[4096]{0:T(1024)S(1)} %bitcast.317), channel_id=1, replica_groups=mesh['row'=4,'col'=8] {'col'}, use_global_device_ids=true, to_apply=%region_36.37 | all-reduce | flops 8192 | bytes 65536 | tf_op jit(solution)/shard_map/psum | solution.py:54
  778.9 6.3 psum.189
  785.8 5.2 all_gather.61
  795.9 5.6 all_gather.62
  807.3 21.0 %fusion.135 = f32[1,4096]{1,0:T(1,128)S(1)} fusion(f32[4096,2048]{0,1:T(8,128)} %subtract_subtract_fusion.1, f32[2048,1]{0,1:T(1,128)S(1)} %bitcast.332), kind=kOutput, calls=%fused_computation.256 | convolution fusion | flops 100663296 | bytes 33579008 | tf_op jit(solution)/shard_map/dot_general | solution.py:19
  828.3 33.0 %psum.190 = f32[4096]{0:T(1024)S(1)} all-reduce(f32[4096]{0:T(1024)S(1)} %bitcast.288), channel_id=1, replica_groups=mesh['row'=4,'col'=8] {'col'}, use_global_device_ids=true, to_apply=%region_40.41 | all-reduce | flops 4096 | bytes 32768 | tf_op jit(solution)/shard_map/psum | solution.py:54
  863.7 6.3 psum.191
  870.6 5.5 all_gather.63
  877.2 30.1 %fusion.11 = f32[4096,2048]{0,1:T(8,128)} fusion(f32[16384,4]{0,1:T(4,128)S(1)} %scatter.76, s32[]{:T(128)S(6)} %select_n.183, f32[16384,4]{0,1:T(4,128)S(1)} %scatter.79, s32[]{:T(128)S(6)} %select_n.184), kind=kOutput, calls=%fused_computation.39 | convolution fusion | flops 402653184 | bytes 33652744 | tf_op jit(solution)/shard_map/dot_general | solution.py:19
  907.3 41.1 %subtract_subtract_fusion = f32[4096,2048]{0,1:T(8,128)} fusion(f32[4096,2048]{0,1:T(8,128)} %subtract_subtract_fusion.1, f32[4096,2048]{0,1:T(8,128)} %fusion.11, f32[16384,4]{0,1:T(4,128)S(1)} %scatter.79, s32[]{:T(128)S(6)} %select_n.183, f32[16384,4]{0,1:T(4,128)S(1)} %scatter.76, s32[]{:T(128)S(6)} %select_n.184), kind=kOutput, calls=%fused_computation | convolution fusion | flops 419430400 | bytes 100761608 | tf_op jit(solution)/shard_map/dot_general | solution.py:19
  948.4 33.3 %copy.49 = f32[4096,2048]{1,0:T(8,128)} copy(f32[4096,2048]{0,1:T(8,128)} %subtract_subtract_fusion) | data formatting | bytes 67108864 | tf_op jit(solution)/shard_map/sub | solution.py:72
  (139 shorter events, 73.5 us)
where the time goes:
time: 991 us; the launch traced here: 982 us
  blocking collectives  472 us (48%)
  matrix products  376 us (38%)
  local copies, waits for them, and re-layouts  87.7 us (9%)
  other arithmetic  24.6 us (2%)
  between operations  22 us (2%)
    dot_general x50, matrix products, product(): jnp.dot(left, right, precision=highest, preferred_element_type=jnp.float32)  376 us
    psum x8, blocking collectives, on_device(): summed = lax.psum(product(current, vector_cols), 'col')  264 us
    psum x2, blocking collectives, from_root(): return lax.psum(kept, axis)  71.8 us
    psum x8, blocking collectives, on_device(): inner = lax.psum(jnp.sum(mapped * vector_rows), 'row')  50.2 us
    all_gather x8, blocking collectives, on_device(): whole = lax.all_gather(column, 'row', axis=0, tiled=True)  43.5 us
    all_gather x8, blocking collectives, on_device(): lax.all_gather(mapped - 0.5 * factor * inner * vector_rows, 'row', axis=0...  42.4 us
    sub x1, local copies, waits for them, and re-layouts, on_device(): current - product(reflector_rows, update_cols.T)  33.3 us
    unnamed x1, local copies, waits for them, and re-layouts  31.1 us

commit v1 on v0

v1 whole, which is shorter than its diff:
```python
import functools

import jax
import jax.numpy as jnp
from jax import lax
from jax.experimental import pallas as pl
from jax.experimental.pallas import tpu as pltpu
from jax.sharding import PartitionSpec as P

REFL = 4
PANELS = 2
STEPS = REFL * PANELS
LANES = 128
MESH = pl.DeviceIdType.MESH


def total_of(value):
    folded = jnp.sum(value, axis=0)
    folded = jnp.sum(folded, axis=0, keepdims=True)
    return jnp.sum(folded, axis=1, keepdims=True)


def kernel(
    nrow, ncol, a_hbm, v_ref, w_ref,
    a_vm, lead, rows, part, prod,
    load_sem, lead_sem,
    lead_send, lead_recv, rows_send, rows_recv,
    part_send, part_recv, prod_send, prod_recv,
):
    rows_local, cols_local = a_vm.shape
    kb = cols_local // LANES
    chunks = load_sem.shape[0]
    chunk = rows_local // chunks
    r = lax.axis_index("row")
    k = lax.axis_index("col")

    lead_load = pltpu.make_async_copy(a_hbm.at[pl.ds(0, STEPS), :], lead, lead_sem)
    lead_load.start()
    loads = []
    for n in range(chunks):
        span = pl.ds(n * chunk, chunk)
        load = pltpu.make_async_copy(a_hbm.at[span, :], a_vm.at[span, :], load_sem.at[n])
        load.start()
        loads.append(load)

    barrier = pltpu.get_barrier_semaphore()
    for d in range(1, nrow):
        pl.semaphore_signal(barrier, inc=1, device_id=(lax.rem(r + d, nrow), k), device_id_type=MESH)
    for d in range(1, ncol):
        pl.semaphore_signal(barrier, inc=1, device_id=(r, lax.rem(k + d, ncol)), device_id_type=MESH)

    v_ref[...] = jnp.zeros_like(v_ref)
    w_ref[...] = jnp.zeros_like(w_ref)
    lead_load.wait()

    @pl.when(r == 0)
    def _():
        for t in range(kb):
            rows[k, :, t, :] = lead[:, t * LANES:(t + 1) * LANES]

    pl.semaphore_wait(barrier, nrow + ncol - 2)

    def lead_copy(peer, n):
        return pltpu.make_async_remote_copy(
            src_ref=rows.at[k], dst_ref=rows.at[k],
            send_sem=lead_send.at[n], recv_sem=lead_recv,
            device_id=(peer, k), device_id_type=MESH,
        )

    @pl.when(r == 0)
    def _():
        for n in range(1, nrow):
            lead_copy(n, n).start()
        for n in range(1, nrow):
            lead_copy(n, n).wait_send()

    @pl.when(r != 0)
    def _():
        lead_copy(0, 0).wait_recv()

    def rows_copy(slot, peer, n):
        return pltpu.make_async_remote_copy(
            src_ref=rows.at[slot], dst_ref=rows.at[slot],
            send_sem=rows_send.at[n], recv_sem=rows_recv.at[slot],
            device_id=(r, peer), device_id_type=MESH,
        )

    for d in range(1, ncol):
        rows_copy(k, lax.rem(k + d, ncol), d).start()
    for d in range(1, ncol):
        rows_copy(k, lax.rem(k + d, ncol), d).wait_send()
        peer = lax.rem(k + ncol - d, ncol)
        rows_copy(peer, peer, d).wait_recv()
    for load in loads:
        load.wait()

    shape = (ncol, kb, LANES)
    positions = (
        lax.broadcasted_iota(jnp.int32, shape, 0) * cols_local
        + lax.broadcasted_iota(jnp.int32, shape, 1) * LANES
        + lax.broadcasted_iota(jnp.int32, shape, 2)
    )
    lane = lax.broadcasted_iota(jnp.int32, (1, LANES), 1)
    groups = rows_local // LANES

    def step(c, carry):
        column = rows[:, c]
        here = lane == c
        for i in range(STEPS):
            wc = jnp.sum(jnp.where(here, w_ref[i, 0, 0:1, :], 0.0), axis=1, keepdims=True)
            vc = jnp.sum(jnp.where(here, v_ref[i, 0, 0:1, :], 0.0), axis=1, keepdims=True)
            column = column - v_ref[i] * wc - w_ref[i] * vc
        beneath = jnp.where(positions > c, column, 0.0)
        leading = total_of(jnp.where(positions == c + 1, column, 0.0))
        length = jnp.sqrt(total_of(beneath * beneath))
        signed = jnp.where(leading >= 0.0, length, -length)
        vector = beneath + jnp.where(positions == c + 1, signed, 0.0)
        factor = 1.0 / (length * (length + jnp.abs(leading)))
        v_ref[c] = vector

        def group(j, sums):
            g = r * groups + j
            piece = v_ref[c, g // kb, pl.ds(g % kb, 1), :]
            spread = jnp.broadcast_to(piece, (LANES, LANES)).T
            base = pl.multiple_of(j * LANES, LANES)
            sums = list(sums)
            for b in range(LANES // 8):
                scale = spread[b * 8:(b + 1) * 8, :]
                for t in range(kb):
                    sums[t] = sums[t] + scale * a_vm[pl.ds(base + b * 8, 8), t * LANES:(t + 1) * LANES]
            return tuple(sums)

        sums = lax.fori_loop(
            0, groups, group, tuple(jnp.zeros((8, LANES), jnp.float32) for _ in range(kb))
        )
        for t in range(kb):
            part[c, r, t:t + 1, :] = jnp.sum(sums[t], axis=0, keepdims=True)

        def part_copy(slot, peer, n):
            return pltpu.make_async_remote_copy(
                src_ref=part.at[c, slot], dst_ref=part.at[c, slot],
                send_sem=part_send.at[n], recv_sem=part_recv.at[c, slot],
                device_id=(peer, k), device_id_type=MESH,
            )

        for d in range(1, nrow):
            part_copy(r, lax.rem(r + d, nrow), d).start()

        fixes = jnp.zeros(shape, jnp.float32)
        w_ref[c] = fixes
        for i in range(STEPS):
            old_v = v_ref[i]
            old_w = w_ref[i]
            fixes = fixes + old_v * total_of(old_w * vector) + old_w * total_of(old_v * vector)

        for d in range(1, nrow):
            peer = lax.rem(r + nrow - d, nrow)
            part_copy(peer, peer, d).wait_recv()
        summed = part[c, 0]
        for n in range(1, nrow):
            summed = summed + part[c, n]
        prod[c, k] = summed

        def prod_copy(slot, peer, n):
            return pltpu.make_async_remote_copy(
                src_ref=prod.at[c, slot], dst_ref=prod.at[c, slot],
                send_sem=prod_send.at[n], recv_sem=prod_recv.at[c, slot],
                device_id=(r, peer), device_id_type=MESH,
            )

        for d in range(1, ncol):
            prod_copy(k, lax.rem(k + d, ncol), d).start()
        for d in range(1, nrow):
            part_copy(r, lax.rem(r + d, nrow), d).wait_send()
        for d in range(1, ncol):
            peer = lax.rem(k + ncol - d, ncol)
            prod_copy(peer, peer, d).wait_recv()
        for d in range(1, ncol):
            prod_copy(k, lax.rem(k + d, ncol), d).wait_send()

        mapped = factor * (prod[c] - fixes)
        inner = total_of(mapped * vector)
        w_ref[c] = mapped - (0.5 * factor * inner) * vector
        return carry

    lax.fori_loop(0, STEPS, step, 0)


def reflectors_of(matrix, nrow, ncol):
    rows_local, cols_local = matrix.shape
    kb = cols_local // LANES
    vectors = jax.ShapeDtypeStruct((STEPS, ncol, kb, LANES), jnp.float32)
    dma = pltpu.SemaphoreType.DMA
    return pl.pallas_call(
        functools.partial(kernel, nrow, ncol),
        out_shape=(vectors, vectors),
        in_specs=[pl.BlockSpec(memory_space=pl.ANY)],
        out_specs=(pl.BlockSpec(memory_space=pltpu.VMEM),) * 2,
        scratch_shapes=[
            pltpu.VMEM((rows_local, cols_local), jnp.float32),
            pltpu.VMEM((STEPS, cols_local), jnp.float32),
            pltpu.VMEM((ncol, STEPS, kb, LANES), jnp.float32),
            pltpu.VMEM((STEPS, nrow, kb, LANES), jnp.float32),
            pltpu.VMEM((STEPS, ncol, kb, LANES), jnp.float32),
            dma((8,)), dma(()),
            dma((nrow,)), dma(()), dma((ncol,)), dma((ncol,)),
            dma((nrow,)), dma((STEPS, nrow)), dma((ncol,)), dma((STEPS, ncol)),
        ],
        compiler_params=pltpu.CompilerParams(
            collective_id=0, has_side_effects=True, vmem_limit_bytes=52 * 1024 * 1024
        ),
    )(matrix)


def thirds(value):
    first = lax.reduce_precision(value, 8, 7)
    rest = value - first
    second = lax.reduce_precision(rest, 8, 7)
    third = rest - second
    return [x.astype(jnp.bfloat16) for x in (first, second, third)]


def on_device(matrix):
    rows_local, cols_local = matrix.shape
    nrow, ncol = lax.axis_size("row"), lax.axis_size("col")
    reflectors, updates = reflectors_of(matrix, nrow, ncol)
    row_start = lax.axis_index("row") * rows_local
    flat_v = reflectors.reshape(STEPS, -1)
    flat_w = updates.reshape(STEPS, -1)
    left = jnp.concatenate([flat_v, flat_w], axis=0)
    left = lax.dynamic_slice_in_dim(left, row_start, rows_local, 1)
    col = lax.axis_index("col")
    right = jnp.concatenate(
        [lax.dynamic_index_in_dim(x, col, 1, keepdims=False).reshape(STEPS, cols_local)
         for x in (updates, reflectors)], axis=0)
    l1, l2, l3 = thirds(left)
    r1, r2, r3 = thirds(right)
    lefts = jnp.concatenate([l1, l1, l2, l2, l1, l3], axis=0)
    rights = jnp.concatenate([r1, r2, r1, r2, r3, r1], axis=0)
    change = lax.dot_general(
        lefts, rights, (((0,), (0,)), ((), ())), preferred_element_type=jnp.float32
    )
    return matrix - change


def solution(mesh):
    return jax.shard_map(
        on_device,
        mesh=mesh,
        in_specs=(P("row", "col"),),
        out_specs=P("row", "col"),
        check_vma=False,
    )
```

time: 991 us -> 150 us (0.15)
  blocking collectives: 472 us -> 0 us
  matrix products: 376 us -> 24.9 us
  Pallas kernels: 0 us -> 124 us
  local copies, waits for them, and re-layouts: 87.7 us -> 0.68 us
  other arithmetic: 24.6 us -> 0.25 us
  between operations: 22 us -> 0.13 us
    psum x18 -> x0, blocking collectives: 387 us -> none  [the longest x8 264 us: on_device(): summed = lax.psum(product(current, vector_cols), 'col')]
    dot_general x50 -> x1, matrix products: 376 us -> 24.9 us  [on_device(): lax.dot_general(lefts, rights, (((0,), (0,)), ((), ())), preferred_elemen...]
    pallas_call x0 -> x1, Pallas kernels: none -> 124 us  [reflectors_of(): pl.pallas_call(functools.partial(kernel, nrow, ncol), out_shape=(vectors,...]
    all_gather x16 -> x0, blocking collectives: 85.8 us -> none  [the longest x8 43.5 us: on_device(): whole = lax.all_gather(column, 'row', axis=0, tiled=True)]
    sub x1 -> x0, local copies, waits for them, and re-layouts: 33.3 us -> none  [on_device(): current - product(reflector_rows, update_cols.T)]
    unnamed x1 -> x2, local copies, waits for them, and re-layouts: 31.1 us -> 0.04 us
    scatter x16 -> x0, local copies, waits for them, and re-layouts: 14.2 us -> none  [the longest x8 7.16 us: on_device(): reflectors = reflectors.at[:, inner_index].set(vector)]
    reduce_sum x16 -> x0, other arithmetic: 10.7 us -> none  [the longest x8 5.54 us: on_device(): inner = lax.psum(jnp.sum(mapped * vector_rows), 'row')]
where the time goes in v1:
time: 150 us
  Pallas kernels  124 us (83%)
  matrix products  24.9 us (17%)
    pallas_call x1, Pallas kernels, reflectors_of(): pl.pallas_call(functools.partial(kernel, nrow, ncol), out_shape=(vectors,...  124 us
    dot_general x1, matrix products, on_device(): lax.dot_general(lefts, rights, (((0,), (0,)), ((), ())), preferred_elemen...  24.9 us

profile of v1, /device:TPU:0, one launch (start us, length us, event | category | flops | bytes accessed | tf_op | source)
XLA Modules:
  0.0 149.9 jit_solution(11005050922915818735)
XLA Ops:
  0.0 123.9 %shard_map.17 = (f32[8,8,16,128]{3,2,1,0:T(8,128)S(1)}, f32[8,8,16,128]{3,2,1,0:T(8,128)S(1)}) custom-call(f32[4096,2048]{1,0:T(8,128)} %a_hbm.1), custom_call_target="tpu_custom_call" | custom-call | tf_op jit(solution)/shard_map/pallas_call | solution.py:194
  124.1 0.6 copy_bitcast_fusion
  125.0 24.9 %convolution_subtract_fusion = f32[4096,2048]{1,0:T(8,128)} fusion(f32[4096,2048]{1,0:T(8,128)} %a_hbm.1, bf16[96,4096]{1,0:T(8,128)(2,1)S(1)} %fusion.3, bf16[96,2048]{1,0:T(8,128)(2,1)S(1)} %constant_dynamic-update-slice_fusion.5), kind=kOutput, calls=%fused_computation | convolution fusion | flops 1619001344 | bytes 68288512 | tf_op jit(solution)/shard_map/dot_general | solution.py:240
  (15 shorter events, 0.3 us)
